TPU v7x, 32 devices: a whole 2x2x4 slice. The times are simulated.
32 devices in a mesh: py: 8 (over z, x), px: 4 (over y, core).
Axes of the slice: x: 2, y: 2, z: 4, core: 2. Of those that a mesh axis runs over, the one named last changes fastest.
Arguments:
- density: float32 [256, 128, 128], P('py', 'px'), may hold values from 0.5 to 2
- conductance: float32 [256, 128, 128], P('py', 'px'), may hold values from 0.03 to 0.22
- source: float32 [256, 128, 128], P('py', 'px'), may hold values from -0.2 to 0.2
Outputs:
- anomaly: float32 [256, 128, 128], P('py', 'px')
- density_end: float32 [256, 128, 128], P('py', 'px')
All inputs are finite; a program needn't handle non-finite values.
Results may differ from a plain program's by a relative error of at most 0.00002.
Values sent between devices are 32-bit elements; how exact they have to be, the bound alone decides.
A program may use at most 64 MiB of HBM per device.

v0:
```python
import functools

import jax
import jax.numpy as jnp
from jax import lax
from jax.experimental import pallas as pl
from jax.experimental.pallas import tpu as pltpu
from jax.sharding import PartitionSpec as P

ROUNDS = (3, 3)
DEEP = max(ROUNDS)
PAD = 4
DIRECTIONS = [(-1, -1), (-1, 1), (1, -1), (1, 1), (-1, 0), (1, 0), (0, -1), (0, 1)]
MESH = pl.DeviceIdType.MESH


def edge(direction, size, depth, own):
    if direction < 0:
        return (own, depth), (own + size, depth)
    if direction > 0:
        return (own + size - depth, depth), (own - depth, depth)
    return (own, size), (own, size)


def kernel(py, px, inner, field, conductance, source, density_out, mean_out, scale_out,
           padded, work, coefficients, stats, local_sem, send_sem, recv_sem, stat_send, stat_recv):
    rows, columns, levels = field.shape
    width = columns + 2 * PAD
    my, mx = lax.axis_index("py"), lax.axis_index("px")

    def exists(dy, dx):
        here = jnp.bool_(True)
        if dy:
            here = here & ((my > 0) if dy < 0 else (my < py - 1))
        if dx:
            here = here & ((mx > 0) if dx < 0 else (mx < px - 1))
        return here

    block = (pl.ds(DEEP, rows), pl.ds(PAD, columns))
    loads = []
    for i, (src, dst) in enumerate(
        [(field, padded.at[0]), (conductance, coefficients.at[0]), (source, coefficients.at[1])]
    ):
        loads.append(pltpu.make_async_copy(src, dst.at[block], local_sem.at[i]))
        loads[-1].start()

    barrier = pltpu.get_barrier_semaphore()
    expected = jnp.int32(py - 1)
    for step in range(1, py):
        pl.semaphore_signal(barrier, 1, device_id=(lax.rem(my + step, py), mx), device_id_type=MESH)
    for dy, dx in DIRECTIONS:
        if dx:
            there = exists(dy, dx)
            expected = expected + there.astype(jnp.int32)

            @pl.when(there)
            def _():
                pl.semaphore_signal(barrier, 1, device_id=(my + dy, mx + dx), device_id_type=MESH)

    holders = [padded.at[r] for r in range(len(ROUNDS))] + [coefficients.at[0], coefficients.at[1]]
    for dim, direction in ((0, -1), (0, 1), (1, -1), (1, 1)):
        outside = ~exists(*((direction, 0) if dim == 0 else (0, direction)))

        @pl.when(outside)
        def _():
            for holder in holders:
                if dim == 0:
                    start = 0 if direction < 0 else DEEP + rows
                    holder[pl.ds(start, DEEP)] = jnp.zeros((DEEP, width, levels), jnp.float32)
                else:
                    start = 0 if direction < 0 else PAD + columns
                    holder[:, pl.ds(start, PAD)] = jnp.zeros((rows + 2 * DEEP, PAD, levels), jnp.float32)

    pl.semaphore_wait(barrier, expected)

    def exchange(number, arrays):
        for d, (dy, dx) in enumerate(DIRECTIONS):
            copies = []
            for a, (src, row0, column0, dst, depth) in enumerate(arrays):
                reach = depth - 1 if dy and dx else depth
                if reach < 1:
                    continue
                (y_from, y_size), _ = edge(dy, rows, reach, row0)
                (x_from, x_size), _ = edge(dx, columns, reach, column0)
                _, (y_to, _) = edge(dy, rows, reach, DEEP)
                _, (x_to, _) = edge(dx, columns, reach, PAD)
                both = (slice(None),) * (len(src.shape) - 3)
                copies.append(
                    pltpu.make_async_remote_copy(
                        src_ref=src.at[both + (pl.ds(y_from, y_size), pl.ds(x_from, x_size))],
                        dst_ref=dst.at[both + (pl.ds(y_to, y_size), pl.ds(x_to, x_size))],
                        send_sem=send_sem.at[number, a, d],
                        recv_sem=recv_sem.at[number, a, d],
                        device_id=(my + dy, mx + dx),
                        device_id_type=MESH,
                    )
                )
            yield (dy, dx), copies

    def start(copies):
        for (dy, dx), group in copies:
            @pl.when(exists(dy, dx))
            def _():
                for copy in group:
                    copy.start()

    def wait_recv(copies):
        for (dy, dx), group in copies:
            @pl.when(exists(-dy, -dx))
            def _():
                for copy in group:
                    copy.wait_recv()

    def wait_send(copies):
        for (dy, dx), group in copies:
            @pl.when(exists(dy, dx))
            def _():
                for copy in group:
                    copy.wait_send()

    tall = rows + 2 * DEEP
    flat_conductance = coefficients.at[0].reshape(tall * width, levels)
    flat_source = coefficients.at[1].reshape(tall * width, levels)

    def advance(old, first, count, column, wide, put, carry):
        flat = old.reshape(tall * width, levels)

        def row(i, state):
            above, middle, carry = state
            at = (first + i) * width + column
            below = flat[pl.ds(at + width, wide), :]
            sides = flat[pl.ds(at - 1, wide), :] + flat[pl.ds(at + 1, wide), :]
            spread = (above + below) + sides - 4.0 * middle
            later = middle + flat_conductance[pl.ds(at, wide), :] * spread + flat_source[pl.ds(at, wide), :]
            return middle, below, put(first - DEEP + i, later, carry)

        at = first * width + column
        state = (flat[pl.ds(at - width, wide), :], flat[pl.ds(at, wide), :], carry)
        return lax.fori_loop(0, count, row, state, unroll=min(count, 4))[2]

    total = jnp.zeros((columns, levels), jnp.float32)
    waiting = []
    for number, steps in enumerate(ROUNDS):
        if number == 0:
            arrays = [
                (padded.at[0], DEEP, PAD, padded.at[0], steps),
                (coefficients, DEEP, PAD, coefficients, DEEP - 1),
            ]
        else:
            arrays = [(padded.at[number], DEEP, PAD, padded.at[number], steps)]
        copies = list(exchange(number, arrays))
        if number == 0:
            for copy in loads:
                copy.wait()
        start(copies)
        waiting.append(copies)
        across = [copy for copy in copies if not copy[0][0]]
        wait_recv(across)
        for part in ("inside", "low", "high"):
            if part != "inside":
                sent = 1 if part == "low" else -1
                wait_recv([copy for copy in copies if copy[0][0] == sent])
            old = padded.at[number]
            for step in range(steps):
                margin = steps - 1 - step
                if part == "inside":
                    spans = [(DEEP + step + 1, rows - 2 * (step + 1))]
                elif part == "low":
                    spans = [(DEEP - margin, steps)]
                else:
                    spans = [(DEEP + rows - step - 1, steps)]
                column, wide, new = PAD, columns, None
                if margin:
                    column, wide, new = 0, width, work.at[step]
                elif number < len(ROUNDS) - 1:
                    new = padded.at[number + 1]

                def put(i, later, carry, new=new, column=column, wide=wide):
                    if new is None:
                        density_out[i] = later
                        return carry + later
                    new.reshape(tall * width, levels)[pl.ds((DEEP + i) * width + column, wide), :] = later
                    return carry

                for first, count in spans:
                    total = advance(old, first, count, column, wide, put, total)
                old = new

    local_mean = total * (1.0 / rows)

    def square(i, carry):
        away = density_out[i] - local_mean
        return carry + away * away

    squares = lax.fori_loop(0, rows, square, jnp.zeros((columns, levels), jnp.float32), unroll=4)
    stats[0, 0] = local_mean
    stats[0, 1] = squares
    outer = py // inner
    far_first = sorted(
        ((do, di) for do in range(outer) for di in range(inner) if do or di),
        key=lambda place: -(min(place[0], outer - place[0]) + min(place[1], inner - place[1])),
    )
    sums = []
    for do, di in far_first:
        step = do * inner + di
        peer = lax.rem(my // inner + do, outer) * inner + lax.rem(lax.rem(my, inner) + di, inner)
        copy = pltpu.make_async_remote_copy(
            src_ref=stats.at[0],
            dst_ref=stats.at[step],
            send_sem=stat_send.at[step],
            recv_sem=stat_recv.at[step],
            device_id=(peer, mx),
            device_id_type=MESH,
        )
        copy.start()
        sums.append(copy)
    for copies in waiting:
        wait_send(copies)
    for copy in sums:
        copy.wait_recv()
    mean = stats[0, 0]
    for step in range(1, py):
        mean = mean + stats[step, 0]
    mean = mean * (1.0 / py)
    inside = stats[0, 1]
    between = (stats[0, 0] - mean) * (stats[0, 0] - mean)
    for step in range(1, py):
        inside = inside + stats[step, 1]
        between = between + (stats[step, 0] - mean) * (stats[step, 0] - mean)
    variance = inside * (1.0 / (rows * py)) + between * (1.0 / py)
    mean_out[...] = mean
    scale_out[...] = lax.rsqrt(variance + 0.0001)
    for copy in sums:
        copy.wait_send()

CHUNKS = 2


def finish(density, mean, scale, anomaly_out, density_out, anomaly, sem):
    rows = density.shape[0]
    whole = pltpu.make_async_copy(density, density_out, sem.at[CHUNKS])
    whole.start()
    part = rows // CHUNKS
    copies = []
    for chunk in range(CHUNKS):
        for i in range(chunk * part, (chunk + 1) * part):
            anomaly[i] = (density[i] - mean[...]) * scale[...]
        own = pl.ds(chunk * part, part)
        copies.append(pltpu.make_async_copy(anomaly.at[own], anomaly_out.at[own], sem.at[chunk]))
        copies[-1].start()
    for copy in copies:
        copy.wait()
    whole.wait()


def per_device(py, px, inner, density, conductance, source):
    rows, columns, levels = density.shape
    tall, width = rows + 2 * DEEP, columns + 2 * PAD
    vmem = pl.BlockSpec(memory_space=pltpu.VMEM)
    line = jax.ShapeDtypeStruct((columns, levels), jnp.float32)
    density, conductance, source = (pltpu.with_memory_space_constraint(x, pltpu.HBM) for x in (density, conductance, source))
    density, mean, scale = pl.pallas_call(
        functools.partial(kernel, py, px, inner),
        out_shape=[jax.ShapeDtypeStruct(density.shape, jnp.float32), line, line],
        in_specs=[pl.BlockSpec(memory_space=pltpu.HBM)] * 3,
        out_specs=[vmem] * 3,
        scratch_shapes=[
            pltpu.VMEM((len(ROUNDS), tall, width, levels), jnp.float32),
            pltpu.VMEM((DEEP - 1, tall, width, levels), jnp.float32),
            pltpu.VMEM((2, tall, width, levels), jnp.float32),
            pltpu.VMEM((py, 2, columns, levels), jnp.float32),
            pltpu.SemaphoreType.DMA((3,)),
            pltpu.SemaphoreType.DMA((len(ROUNDS), 3, len(DIRECTIONS))),
            pltpu.SemaphoreType.DMA((len(ROUNDS), 3, len(DIRECTIONS))),
            pltpu.SemaphoreType.DMA((py,)),
            pltpu.SemaphoreType.DMA((py,)),
        ],
        compiler_params=pltpu.CompilerParams(collective_id=0, has_side_effects=True, vmem_limit_bytes=10*2**20),
    )(density, conductance, source)
    return pl.pallas_call(
        finish,
        out_shape=[jax.ShapeDtypeStruct(density.shape, jnp.float32)] * 2,
        in_specs=[vmem] * 3,
        out_specs=[pl.BlockSpec(memory_space=pltpu.HBM)] * 2,
        scratch_shapes=[pltpu.VMEM(density.shape, jnp.float32), pltpu.SemaphoreType.DMA((CHUNKS + 1,))],
        compiler_params=pltpu.CompilerParams(vmem_limit_bytes=4 * 2**20),
    )(density, mean, scale)


def solution(mesh):
    spec = P("py", "px", None)
    line = mesh.devices.reshape(mesh.shape["py"], -1)[:, 0] if mesh.axis_names[0] == "py" else []
    places = [getattr(device, "coords", (0, 0, 0))[2] for device in line]
    inner = max(1, places.count(places[0])) if places else 1
    return jax.shard_map(
        functools.partial(per_device, mesh.shape["py"], mesh.shape["px"], inner),
        mesh=mesh, in_specs=(spec,) * 3, out_specs=(spec,) * 2, check_vma=False,
    )
```

profile of v0, /device:TPU:0, one launch (start us, length us, event | category | flops | bytes accessed | tf_op | source)
XLA Modules:
  0.0 26.1 jit_solution(8012177322114492861)
XLA Ops:
  0.6 24.5 %shard_map.50 = (f32[32,32,128]{2,1,0:T(8,128)S(1)}, f32[32,128]{1,0:T(8,128)S(1)}, f32[32,128]{1,0:T(8,128)S(1)}) custom-call(f32[32,32,128]{2,1,0:T(8,128)} %field.1, f32[32,32,128]{2,1,0:T(8,128)} %conductance.1, f32[32,32,128]{2,1,0:T(8,128)} %source.1), custom_call_target="tpu_custom_call" | custom-call | tf_op jit(solution)/shard_map/pallas_call | solution.py:262
  25.1 1.0 %shard_map.51 = (f32[32,32,128]{2,1,0:T(8,128)}, f32[32,32,128]{2,1,0:T(8,128)}) custom-call(f32[32,32,128]{2,1,0:T(8,128)S(1)} %get-tuple-element.5.density, f32[32,128]{1,0:T(8,128)S(1)} %get-tuple-element.6.mean, f32[32,128]{1,0:T(8,128)S(1)} %get-tuple-element.7.scale), custom_call_target="tpu_custom_call" | custom-call | tf_op jit(solution)/shard_map/pallas_call | solution.py:280
where the time goes:
time: 26.3 us; the launch traced here: 26.1 us
  Pallas kernels  25.5 us (97%)
  between operations  0.64 us (2%)
    pallas_call x1, Pallas kernels, per_device(): pl.pallas_call(functools.partial(kernel, py, px, inner), out_shape=[jax.S...  24.5 us
    pallas_call x1, Pallas kernels, per_device(): pl.pallas_call(finish, out_shape=[jax.ShapeDtypeStruct(density.shape, jnp...  0.99 us

commit v1 on v0

v1 whole, which is shorter than its diff:
```python
import functools

import jax
import jax.numpy as jnp
from jax import lax
from jax.experimental import pallas as pl
from jax.experimental.pallas import tpu as pltpu
from jax.sharding import PartitionSpec as P

ROUNDS = 2
DEEP = 3
PAD = 4
TOP = 2
DIRECTIONS = [(-1, 0), (1, 0), (-1, -1), (-1, 1), (1, -1), (1, 1), (0, -1), (0, 1)]
MESH = pl.DeviceIdType.MESH


def kernel(py, px, inner, field, conductance, source, density_out, mean_out, scale_out,
           padded, work, coefficients, ready, extra, stats, local_sem, send_sem, recv_sem,
           stat_send, stat_recv, present):
    rows, columns, levels = field.shape
    width = columns + 2 * PAD
    tall = rows + 2 * TOP
    my, mx = lax.axis_index("py"), lax.axis_index("px")

    def exists(dy, dx):
        here = jnp.bool_(True)
        if dy:
            here = here & ((my + dy >= 0) if dy < 0 else (my + dy < py))
        if dx:
            here = here & ((mx + dx >= 0) if dx < 0 else (mx + dx < px))
        return here

    own = pl.ds(PAD, columns)
    block = (pl.ds(TOP, rows), own)
    loads = []
    for i, (src, dst) in enumerate(
        [(field, padded.at[0]), (conductance, coefficients.at[0]), (source, coefficients.at[1])]
    ):
        loads.append(pltpu.make_async_copy(src, dst.at[block], local_sem.at[i]))
        loads[-1].start()

    barrier = pltpu.get_barrier_semaphore()
    expected = jnp.int32(0)
    for dy, dx in DIRECTIONS:
        there = exists(dy, dx)
        expected = expected + there.astype(jnp.int32)

        @pl.when(there)
        def _():
            pl.semaphore_signal(barrier, 1, device_id=(my + dy, mx + dx), device_id_type=MESH)

    holders = [padded.at[r] for r in range(ROUNDS)] + [coefficients.at[0], coefficients.at[1]]
    for side, dy in enumerate((-1, 1)):
        @pl.when(~exists(dy, 0))
        def _():
            for holder in holders[:-1]:
                start = 0 if dy < 0 else TOP + rows
                holder[pl.ds(start, TOP)] = jnp.zeros((TOP, width, levels), jnp.float32)
            for number in range(ROUNDS):
                extra[number, side] = jnp.zeros((2, width, levels), jnp.float32)
    for dx in (-1, 1):
        @pl.when(~exists(0, dx))
        def _():
            start = pl.ds(0 if dx < 0 else PAD + columns, PAD)
            for holder in holders:
                holder[:, start] = jnp.zeros((tall, PAD, levels), jnp.float32)
            for number in range(ROUNDS):
                for side in range(2):
                    extra[number, side, :, start] = jnp.zeros((2, PAD, levels), jnp.float32)

    pl.semaphore_wait(barrier, expected)

    edges = (TOP, TOP + rows - 1)
    beyond = (TOP - 1, TOP + rows)

    def remote(number, slot, direction, src, dst):
        d = DIRECTIONS.index(direction)
        return direction, pltpu.make_async_remote_copy(
            src_ref=src,
            dst_ref=dst,
            send_sem=send_sem.at[number, slot, d],
            recv_sem=recv_sem.at[number, slot, d],
            device_id=(my + direction[0], mx + direction[1]),
            device_id_type=MESH,
        )

    def start(copies):
        for (dy, dx), copy in copies:
            @pl.when(exists(dy, dx))
            def _():
                copy.start()

    def wait_recv(copies):
        for (dy, dx), copy in copies:
            @pl.when(exists(-dy, -dx))
            def _():
                copy.wait_recv()

    def wait_send(copies):
        for (dy, dx), copy in copies:
            @pl.when(exists(dy, dx))
            def _():
                copy.wait_send()

    def raw_rows(number, dy):
        side = 0 if dy < 0 else 1
        edge, far = edges[side], beyond[1 - side]
        second, far_second = edge - dy, far - dy
        out = [remote(number, 0, (dy, 0), padded.at[number, edge, own], padded.at[number, far, own])]
        if number == 0:
            out.append(remote(number, 1, (dy, 0), coefficients.at[0, edge, own], coefficients.at[0, far, own]))
            for slot, column in ((3, PAD), (4, PAD + columns - 1)):
                at = pl.ds(column, 1)
                out.append(remote(number, slot, (dy, 0), coefficients.at[0, second, at], coefficients.at[0, far_second, at]))
        for dx in (-1, 1):
            first, last = min(edge, second), min(far, far_second)
            from_ = PAD if dx < 0 else PAD + columns - 2
            to = PAD + columns if dx < 0 else PAD - 2
            out.append(remote(number, 0, (dy, dx), padded.at[number, pl.ds(first, 2), pl.ds(from_, 2)],
                              padded.at[number, pl.ds(last, 2), pl.ds(to, 2)]))
            if number == 0:
                from_ = PAD if dx < 0 else PAD + columns - 1
                to = PAD + columns if dx < 0 else PAD - 1
                out.append(remote(number, 1, (dy, dx), coefficients.at[0, edge, pl.ds(from_, 1)],
                                  coefficients.at[0, far, pl.ds(to, 1)]))
        return out

    def row_terms(number, dy):
        side = 0 if dy < 0 else 1
        out = [remote(number, 2, (dy, 0), ready.at[number, side], extra.at[number, 1 - side, :, own])]
        for dx in (-1, 1):
            from_ = 0 if dx < 0 else columns - 1
            to = PAD + columns if dx < 0 else PAD - 1
            out.append(remote(number, 2, (dy, dx), ready.at[number, side, 0, pl.ds(from_, 1)],
                              extra.at[number, 1 - side, 0, pl.ds(to, 1)]))
        return out

    def make_terms(number, dy):
        side = 0 if dy < 0 else 1
        edge = edges[side]
        second, third = edge - dy, edge - 2 * dy
        middle = padded[number, second, own]
        place = lax.broadcasted_iota(jnp.int32, (columns, levels), 0)
        before = jnp.where(place == 0, 0.0, pltpu.roll(middle, 1, 0))
        after = jnp.where(place == columns - 1, 0.0, pltpu.roll(middle, columns - 1, 0))
        spread = (padded[number, edge, own] + padded[number, third, own]) + (before + after) - 4.0 * middle
        later = middle + coefficients[0, second, own] * spread + coefficients[1, second, own]
        rate, gain = coefficients[0, edge, own], coefficients[1, edge, own]
        ready[number, side, 0] = rate * middle + gain
        ready[number, side, 1] = rate * later + gain

    def sideways(number, slot, first, count):
        out = []
        for dx in (-1, 1):
            arrays = [(padded.at[number], 3)]
            if number == 0:
                arrays += [(coefficients.at[0], 2), (coefficients.at[1], 2)]
            for a, (array, reach) in enumerate(arrays):
                from_ = PAD if dx < 0 else PAD + columns - reach
                to = PAD + columns if dx < 0 else PAD - reach
                out.append(remote(number, slot + a, (0, dx), array.at[pl.ds(first, count), pl.ds(from_, reach)],
                                  array.at[pl.ds(first, count), pl.ds(to, reach)]))
        return out

    flat_conductance = coefficients.at[0].reshape(tall * width, levels)
    flat_source = coefficients.at[1].reshape(tall * width, levels)

    def advance(old, first, count, column, wide, put, carry):
        flat = old.reshape(tall * width, levels)

        def row(i, state):
            above, middle, carry = state
            at = (first + i) * width + column
            below = flat[pl.ds(at + width, wide), :]
            sides = flat[pl.ds(at - 1, wide), :] + flat[pl.ds(at + 1, wide), :]
            spread = (above + below) + sides - 4.0 * middle
            later = middle + flat_conductance[pl.ds(at, wide), :] * spread + flat_source[pl.ds(at, wide), :]
            return middle, below, put(first - TOP + i, later, carry)

        at = first * width + column
        state = (flat[pl.ds(at - width, wide), :], flat[pl.ds(at, wide), :], carry)
        return lax.fori_loop(0, count, row, state, unroll=min(count, 4))[2]

    def advance_beyond(number, side, step, old, new):
        flat = old.reshape(tall * width, levels)
        at = beyond[side] * width
        inward = edges[side] * width
        middle = flat[pl.ds(at, width), :]
        sides = flat[pl.ds(at - 1, width), :] + flat[pl.ds(at + 1, width), :]
        spread = flat[pl.ds(inward, width), :] + sides - 4.0 * middle
        later = middle + flat_conductance[pl.ds(at, width), :] * spread + extra[number, side, step]
        new.reshape(tall * width, levels)[pl.ds(at, width), :] = later

    def mend(number, side):
        outward = 2 * side - 1
        far = beyond[side]
        for column, other in ((PAD, PAD - 1), (PAD + columns - 1, PAD + columns)):
            at, corner = pl.ds(column, 1), pl.ds(other, 1)
            extra[number, side, 1, at] = extra[number, side, 1, at] + (
                coefficients[0, far, at] * coefficients[0, far + outward, at]
            ) * padded[number, far + outward, corner]


    def announce(reach, index):
        for dy in (-reach, reach):
            @pl.when(exists(dy, 0))
            def _():
                pl.semaphore_signal(present.at[index], 1, device_id=(my + dy, mx), device_id_type=MESH)

    def hear(reach, index):
        count = exists(-reach, 0).astype(jnp.int32) + exists(reach, 0).astype(jnp.int32)
        pl.semaphore_wait(present.at[index], count)

    reaches = []
    while 2 ** (len(reaches) + 1) < py - 1:
        reaches.append(2 ** (len(reaches) + 1))

    for copy in loads:
        copy.wait()
    sent = []
    to_sides = [raw_rows(0, -1), raw_rows(0, 1)]
    for group in to_sides:
        start(group)
    for side, dy in enumerate((-1, 1)):
        make_terms(0, dy)
        terms = row_terms(0, dy)
        start(terms)
        to_sides[side] = to_sides[side] + terms
    across = sideways(0, 0, TOP, rows)
    start(across)

    total = jnp.zeros((columns, levels), jnp.float32)
    for number in range(ROUNDS):
        sent += across + to_sides[0] + to_sides[1]
        wait_recv(across)
        if number:
            if reaches:
                hear(reaches[0], 0)
            for index in range(1, min(2, len(reaches))):
                announce(reaches[index], index)
        next_sides, next_across = [], []
        for part in ("inside", "low", "high"):
            side = None if part == "inside" else (0 if part == "low" else 1)
            if side is not None:
                wait_recv(to_sides[1 - side])
                mend(number, side)
            old = padded.at[number]
            for step in range(DEEP):
                last = step == DEEP - 1
                if part == "inside":
                    first, count = TOP + step + 1, rows - 2 * (step + 1)
                elif part == "low":
                    first, count = TOP, step + 1
                else:
                    first, count = TOP + rows - step - 1, step + 1
                column, wide, new = 0, width, None
                if not last:
                    new = work.at[step]
                else:
                    column, wide = PAD, columns
                    if number < ROUNDS - 1:
                        new = padded.at[number + 1]

                def put(i, later, carry, new=new, column=column, wide=wide):
                    if new is None:
                        density_out[i] = later
                        return carry + later
                    new.reshape(tall * width, levels)[pl.ds((TOP + i) * width + column, wide), :] = later
                    return carry

                total = advance(old, first, count, column, wide, put, total)
                if side is not None and not last:
                    advance_beyond(number, side, step, old, new)
                old = new
            if number < ROUNDS - 1:
                if side is None:
                    some = sideways(number + 1, 0, TOP + DEEP, rows - 2 * DEEP)
                    start(some)
                    next_across += some
                else:
                    dy = 2 * side - 1
                    group = raw_rows(number + 1, dy)
                    start(group)
                    make_terms(number + 1, dy)
                    terms = row_terms(number + 1, dy)
                    start(terms)
                    next_sides.append(group + terms)
                    some = sideways(number + 1, 1 + side, TOP if side == 0 else TOP + rows - DEEP, DEEP)
                    start(some)
                    next_across += some
        if number == 0 and reaches:
            announce(reaches[0], 0)
        to_sides, across = next_sides, next_across

    local_mean = total * (1.0 / rows)

    def square(i, carry):
        away = density_out[i] - local_mean
        return carry + away * away

    squares = lax.fori_loop(0, rows, square, jnp.zeros((columns, levels), jnp.float32), unroll=4)
    stats[0, 0] = local_mean
    stats[0, 1] = squares
    for index in range(1, len(reaches)):
        hear(reaches[index], index)
        if index + 1 < len(reaches):
            announce(reaches[index + 1], index + 1)
    outer = py // inner
    far_first = sorted(
        ((do, di) for do in range(outer) for di in range(inner) if do or di),
        key=lambda place: -(min(place[0], outer - place[0]) + min(place[1], inner - place[1])),
    )
    sums = []
    for do, di in far_first:
        step = do * inner + di
        peer = lax.rem(my // inner + do, outer) * inner + lax.rem(lax.rem(my, inner) + di, inner)
        copy = pltpu.make_async_remote_copy(
            src_ref=stats.at[0],
            dst_ref=stats.at[step],
            send_sem=stat_send.at[step],
            recv_sem=stat_recv.at[step],
            device_id=(peer, mx),
            device_id_type=MESH,
        )
        copy.start()
        sums.append(copy)
    wait_send(sent)
    for copy in sums:
        copy.wait_recv()
    mean = stats[0, 0]
    for step in range(1, py):
        mean = mean + stats[step, 0]
    mean = mean * (1.0 / py)
    inside = stats[0, 1]
    between = (stats[0, 0] - mean) * (stats[0, 0] - mean)
    for step in range(1, py):
        inside = inside + stats[step, 1]
        between = between + (stats[step, 0] - mean) * (stats[step, 0] - mean)
    variance = inside * (1.0 / (rows * py)) + between * (1.0 / py)
    mean_out[...] = mean
    scale_out[...] = lax.rsqrt(variance + 0.0001)
    for copy in sums:
        copy.wait_send()

CHUNKS = 2


def finish(density, mean, scale, anomaly_out, density_out, anomaly, sem):
    rows = density.shape[0]
    whole = pltpu.make_async_copy(density, density_out, sem.at[CHUNKS])
    whole.start()
    part = rows // CHUNKS
    copies = []
    for chunk in range(CHUNKS):
        for i in range(chunk * part, (chunk + 1) * part):
            anomaly[i] = (density[i] - mean[...]) * scale[...]
        own = pl.ds(chunk * part, part)
        copies.append(pltpu.make_async_copy(anomaly.at[own], anomaly_out.at[own], sem.at[chunk]))
        copies[-1].start()
    for copy in copies:
        copy.wait()
    whole.wait()


def per_device(py, px, inner, density, conductance, source):
    rows, columns, levels = density.shape
    tall, width = rows + 2 * TOP, columns + 2 * PAD
    vmem = pl.BlockSpec(memory_space=pltpu.VMEM)
    line = jax.ShapeDtypeStruct((columns, levels), jnp.float32)
    density, conductance, source = (pltpu.with_memory_space_constraint(x, pltpu.HBM) for x in (density, conductance, source))
    density, mean, scale = pl.pallas_call(
        functools.partial(kernel, py, px, inner),
        out_shape=[jax.ShapeDtypeStruct(density.shape, jnp.float32), line, line],
        in_specs=[pl.BlockSpec(memory_space=pltpu.HBM)] * 3,
        out_specs=[vmem] * 3,
        scratch_shapes=[
            pltpu.VMEM((ROUNDS, tall, width, levels), jnp.float32),
            pltpu.VMEM((DEEP - 1, tall, width, levels), jnp.float32),
            pltpu.VMEM((2, tall, width, levels), jnp.float32),
            pltpu.VMEM((ROUNDS, 2, 2, columns, levels), jnp.float32),
            pltpu.VMEM((ROUNDS, 2, 2, width, levels), jnp.float32),
            pltpu.VMEM((py, 2, columns, levels), jnp.float32),
            pltpu.SemaphoreType.DMA((3,)),
            pltpu.SemaphoreType.DMA((ROUNDS, 5, len(DIRECTIONS))),
            pltpu.SemaphoreType.DMA((ROUNDS, 5, len(DIRECTIONS))),
            pltpu.SemaphoreType.DMA((py,)),
            pltpu.SemaphoreType.DMA((py,)),
            pltpu.SemaphoreType.REGULAR((8,)),
        ],
        compiler_params=pltpu.CompilerParams(collective_id=0, has_side_effects=True, vmem_limit_bytes=10*2**20),
    )(density, conductance, source)
    return pl.pallas_call(
        finish,
        out_shape=[jax.ShapeDtypeStruct(density.shape, jnp.float32)] * 2,
        in_specs=[vmem] * 3,
        out_specs=[pl.BlockSpec(memory_space=pltpu.HBM)] * 2,
        scratch_shapes=[pltpu.VMEM(density.shape, jnp.float32), pltpu.SemaphoreType.DMA((CHUNKS + 1,))],
        compiler_params=pltpu.CompilerParams(vmem_limit_bytes=4 * 2**20),
    )(density, mean, scale)


def solution(mesh):
    spec = P("py", "px", None)
    line = mesh.devices.reshape(mesh.shape["py"], -1)[:, 0] if mesh.axis_names[0] == "py" else []
    places = [getattr(device, "coords", (0, 0, 0))[2] for device in line]
    inner = max(1, places.count(places[0])) if places else 1
    return jax.shard_map(
        functools.partial(per_device, mesh.shape["py"], mesh.shape["px"], inner),
        mesh=mesh, in_specs=(spec,) * 3, out_specs=(spec,) * 2, check_vma=False,
    )
```

time: 26.3 us -> 25 us (0.951)
  Pallas kernels: 25.5 us -> 24.2 us
    pallas_call x1, Pallas kernels: 24.5 us -> 23.3 us  [per_device(): pl.pallas_call(functools.partial(kernel, py, px, inner), out_shape=[jax.S...]
where the time goes in v1:
time: 25 us; the launch traced here: 24.9 us
  Pallas kernels  24.2 us (97%)
  between operations  0.64 us (3%)
    pallas_call x1, Pallas kernels, per_device(): pl.pallas_call(functools.partial(kernel, py, px, inner), out_shape=[jax.S...  23.3 us
    pallas_call x1, Pallas kernels, per_device(): pl.pallas_call(finish, out_shape=[jax.ShapeDtypeStruct(density.shape, jnp...  0.99 us

profile of v1, /device:TPU:0, one launch (start us, length us, event | category | flops | bytes accessed | tf_op | source)
XLA Modules:
  0.0 24.9 jit_solution(13594851196983058530)
XLA Ops:
  0.6 23.3 %shard_map.50 = (f32[32,32,128]{2,1,0:T(8,128)S(1)}, f32[32,128]{1,0:T(8,128)S(1)}, f32[32,128]{1,0:T(8,128)S(1)}) custom-call(f32[32,32,128]{2,1,0:T(8,128)} %field.1, f32[32,32,128]{2,1,0:T(8,128)} %conductance.1, f32[32,32,128]{2,1,0:T(8,128)} %source.1), custom_call_target="tpu_custom_call" | custom-call | tf_op jit(solution)/shard_map/pallas_call | solution.py:372
  23.9 1.0 %shard_map.51 = (f32[32,32,128]{2,1,0:T(8,128)}, f32[32,32,128]{2,1,0:T(8,128)}) custom-call(f32[32,32,128]{2,1,0:T(8,128)S(1)} %get-tuple-element.5.density, f32[32,128]{1,0:T(8,128)S(1)} %get-tuple-element.6.mean, f32[32,128]{1,0:T(8,128)S(1)} %get-tuple-element.7.scale), custom_call_target="tpu_custom_call" | custom-call | tf_op jit(solution)/shard_map/pallas_call | solution.py:393

commit v2 on v1

v2 whole, which is shorter than its diff:
```python
import functools

import jax
import jax.numpy as jnp
from jax import lax
from jax.experimental import pallas as pl
from jax.experimental.pallas import tpu as pltpu
from jax.sharding import PartitionSpec as P

ROUNDS = 2
DEEP = 3
PAD = 4
TOP = 2
DIRECTIONS = [(-1, 0), (1, 0), (-1, -1), (-1, 1), (1, -1), (1, 1), (0, -1), (0, 1)]
MESH = pl.DeviceIdType.MESH
FIELD = (0, 3)
RATE, GAIN = 1, 2
CORNER = (5, 4)


def reaches_of(py):
    known, reaches = 1, []
    while known < py - 1:
        reaches.append(known)
        known *= 2
    return reaches


def parcel(number, columns):
    return (4 if number == 0 else 3) * columns + (2 if number == 0 else 0)


def kernel(py, px, inner, field, conductance, source, density_out, mean_out, scale_out,
           arrays, work, extra, parcel_out, parcel_in, corner_out, corner_in, stats,
           load_sem, send_sem, side_sem, across_sem, stat_sem, present):
    rows, columns, levels = field.shape
    width = columns + 2 * PAD
    tall = rows + 2 * TOP
    my, mx = lax.axis_index("py"), lax.axis_index("px")
    reaches = reaches_of(py)

    def exists(dy, dx):
        here = jnp.bool_(True)
        if dy:
            here = here & ((my + dy >= 0) if dy < 0 else (my + dy < py))
        if dx:
            here = here & ((mx + dx >= 0) if dx < 0 else (mx + dx < px))
        return here

    own = pl.ds(PAD, columns)
    middle_rows = rows - 2 * DEEP
    inputs = (field, conductance, source)
    for first, count, group in ((0, DEEP, 0), (rows - DEEP, DEEP, 0), (DEEP, middle_rows, 1)):
        for i, src in enumerate(inputs):
            pltpu.make_async_copy(
                src.at[pl.ds(first, count)], arrays.at[i, pl.ds(TOP + first, count), own], load_sem.at[group]
            ).start()

    barrier = pltpu.get_barrier_semaphore()
    expected = jnp.int32(0)
    for dy, dx in DIRECTIONS:
        there = exists(dy, dx)
        expected = expected + there.astype(jnp.int32)

        @pl.when(there)
        def _():
            pl.semaphore_signal(barrier, 1, device_id=(my + dy, mx + dx), device_id_type=MESH)

    for side, dy in enumerate((-1, 1)):
        @pl.when(~exists(dy, 0))
        def _():
            for number in range(ROUNDS):
                parcel_in[number, side] = jnp.zeros(parcel_in.shape[2:], jnp.float32)
        for other, dx in enumerate((-1, 1)):
            @pl.when(~exists(dy, dx))
            def _():
                for number in range(ROUNDS):
                    corner_in[number, side, other] = jnp.zeros(corner_in.shape[3:], jnp.float32)
    for dx in (-1, 1):
        @pl.when(~exists(0, dx))
        def _():
            start = pl.ds(0 if dx < 0 else PAD + columns, PAD)
            for i in range(4):
                arrays[i, pl.ds(TOP, rows), start] = jnp.zeros((rows, PAD, levels), jnp.float32)

    edges = (TOP, TOP + rows - 1)
    beyond = (TOP - 1, TOP + rows)

    def prepare(number, side):
        at = FIELD[number]
        edge, inward = edges[side], 1 - 2 * side
        second, third = edge + inward, edge + 2 * inward
        outer, middle = arrays[at, edge, own], arrays[at, second, own]
        place = lax.broadcasted_iota(jnp.int32, (columns, levels), 0)
        before = jnp.where(place == 0, 0.0, pltpu.roll(middle, 1, 0))
        after = jnp.where(place == columns - 1, 0.0, pltpu.roll(middle, columns - 1, 0))
        spread = (outer + arrays[at, third, own]) + (before + after) - 4.0 * middle
        second_rate = arrays[RATE, second, own]
        later = middle + second_rate * spread + arrays[GAIN, second, own]
        rate, gain = arrays[RATE, edge, own], arrays[GAIN, edge, own]
        term = rate * middle + gain
        out = parcel_out.at[number, side]
        out[pl.ds(0, columns)] = outer
        out[pl.ds(columns, columns)] = term
        out[pl.ds(2 * columns, columns)] = rate * later + gain
        if number == 0:
            out[pl.ds(3 * columns, columns)] = rate
            out[pl.ds(4 * columns, 1)] = second_rate[:1]
            out[pl.ds(4 * columns + 1, 1)] = second_rate[columns - 1:]
        for other in range(2):
            last = columns - 1 if other else 0
            beside = columns - 2 if other else 1
            cells = corner_out.at[number, side, other]
            cells[pl.ds(0, 1)] = outer[last:last + 1]
            cells[pl.ds(1, 1)] = outer[beside:beside + 1]
            cells[pl.ds(2, 1)] = middle[last:last + 1]
            cells[pl.ds(3, 1)] = term[last:last + 1]
            if number == 0:
                cells[pl.ds(4, 1)] = rate[last:last + 1]

    def remote(direction, src, dst, recv):
        return direction, pltpu.make_async_remote_copy(
            src_ref=src,
            dst_ref=dst,
            send_sem=send_sem.at[DIRECTIONS.index(direction)],
            recv_sem=recv,
            device_id=(my + direction[0], mx + direction[1]),
            device_id_type=MESH,
        )

    def to_side(number, side):
        dy, there = 2 * side - 1, 1 - side
        out = []
        for other, dx in enumerate((-1, 1)):
            cells = pl.ds(0, CORNER[number])
            out.append(remote((dy, dx), corner_out.at[number, side, other, cells],
                              corner_in.at[number, there, 1 - other, cells], side_sem.at[number, there, 2 - other]))
        size = pl.ds(0, parcel(number, columns))
        out.append(remote((dy, 0), parcel_out.at[number, side, size], parcel_in.at[number, there, size],
                          side_sem.at[number, there, 0]))
        return out

    def start(copies):
        for (dy, dx), copy in copies:
            @pl.when(exists(dy, dx))
            def _():
                copy.start()

    def wait_side(number, side):
        for (dy, dx), copy in to_side(number, 1 - side):
            @pl.when(exists(-dy, -dx))
            def _():
                copy.wait_recv()

    def sideways(number, first, count):
        out = []
        for other, dx in enumerate((-1, 1)):
            for i, reach in ((FIELD[number], 3),) + (((RATE, 2), (GAIN, 2)) if number == 0 else ()):
                from_ = PAD if dx < 0 else PAD + columns - reach
                to = PAD + columns if dx < 0 else PAD - reach
                out.append(remote((0, dx), arrays.at[i, pl.ds(first, count), pl.ds(from_, reach)],
                                  arrays.at[i, pl.ds(first, count), pl.ds(to, reach)], across_sem.at[number, 1 - other]))
        return out

    flat_all = arrays.reshape(4 * tall * width, levels)

    def settle(sem, count):
        some = flat_all.at[pl.ds(0, count)]
        pltpu.make_async_copy(some, some, sem).wait()

    def wait_across(number):
        for other, dx in enumerate((-1, 1)):
            @pl.when(exists(0, dx))
            def _():
                settle(across_sem.at[number, other], rows * (7 if number == 0 else 3))

    flat_rate = arrays.at[RATE].reshape(tall * width, levels)
    flat_gain = arrays.at[GAIN].reshape(tall * width, levels)

    def advance(old, first, count, column, wide, put, carry):
        flat = old.reshape(tall * width, levels)

        def row(i, state):
            above, middle, carry = state
            at = (first + i) * width + column
            below = flat[pl.ds(at + width, wide), :]
            sides = flat[pl.ds(at - 1, wide), :] + flat[pl.ds(at + 1, wide), :]
            spread = (above + below) + sides - 4.0 * middle
            later = middle + flat_rate[pl.ds(at, wide), :] * spread + flat_gain[pl.ds(at, wide), :]
            return middle, below, put(first - TOP + i, later, carry)

        at = first * width + column
        state = (flat[pl.ds(at - width, wide), :], flat[pl.ds(at, wide), :], carry)
        return lax.fori_loop(0, count, row, state, unroll=min(count, 4))[2]

    def advance_beyond(side, step, old, new):
        flat = old.reshape(tall * width, levels)
        at = beyond[side] * width
        inward = edges[side] * width
        middle = flat[pl.ds(at, width), :]
        sides = flat[pl.ds(at - 1, width), :] + flat[pl.ds(at + 1, width), :]
        spread = flat[pl.ds(inward, width), :] + sides - 4.0 * middle
        later = middle + flat_rate[pl.ds(at, width), :] * spread + extra[side, step]
        new.reshape(tall * width, levels)[pl.ds(at, width), :] = later

    def unpack(number, side):
        at, far = FIELD[number], beyond[side]
        came = parcel_in.at[number, side]
        arrays[at, far, own] = came[pl.ds(0, columns)]
        extra[side, 0, own] = came[pl.ds(columns, columns)]
        extra[side, 1, own] = came[pl.ds(2 * columns, columns)]
        if number == 0:
            arrays[RATE, far, own] = came[pl.ds(3 * columns, columns)]
        for other in range(2):
            cells = corner_in.at[number, side, other]
            last = pl.ds(PAD + columns - 1 if other else PAD, 1)
            near = pl.ds(PAD + columns if other else PAD - 1, 1)
            next_ = pl.ds(PAD + columns + 1 if other else PAD - 2, 1)
            arrays[at, far, near] = cells[pl.ds(0, 1)]
            arrays[at, far, next_] = cells[pl.ds(1, 1)]
            extra[side, 0, near] = cells[pl.ds(3, 1)]
            if number == 0:
                arrays[RATE, far, near] = cells[pl.ds(4, 1)]
            second_rate = parcel_in[0, side, pl.ds(4 * columns + other, 1)]
            extra[side, 1, last] = extra[side, 1, last] + (arrays[RATE, far, last] * second_rate) * cells[pl.ds(2, 1)]

    def announce(index):
        if index < len(reaches):
            for dy in (-reaches[index], reaches[index]):
                @pl.when(exists(dy, 0))
                def _():
                    pl.semaphore_signal(present.at[index], 1, device_id=(my + dy, mx), device_id_type=MESH)

    def hear(index):
        if index < len(reaches):
            count = exists(-reaches[index], 0).astype(jnp.int32) + exists(reaches[index], 0).astype(jnp.int32)
            pl.semaphore_wait(present.at[index], count)

    settle(load_sem.at[0], 3 * 2 * DEEP * columns)
    for side in range(2):
        prepare(0, side)
    pl.semaphore_wait(barrier, expected)
    for side in range(2):
        start(to_side(0, side))
    announce(0)
    settle(load_sem.at[1], 3 * middle_rows * columns)
    start(sideways(0, TOP, rows))

    total = jnp.zeros((columns, levels), jnp.float32)
    for number in range(ROUNDS):
        wait_across(number)
        hear(2 * number)
        announce(2 * number + 1)
        for part in ("inside", "low", "high"):
            side = None if part == "inside" else (0 if part == "low" else 1)
            if side is not None:
                wait_side(number, side)
                unpack(number, side)
            old = arrays.at[FIELD[number]]
            for step in range(DEEP):
                last = step == DEEP - 1
                if part == "inside":
                    first, count = TOP + step + 1, rows - 2 * (step + 1)
                elif part == "low":
                    first, count = TOP, step + 1
                else:
                    first, count = TOP + rows - step - 1, step + 1
                column, wide, new = 0, width, None
                if not last:
                    new = work.at[step]
                else:
                    column, wide = PAD, columns
                    if number < ROUNDS - 1:
                        new = arrays.at[FIELD[number + 1]]

                def put(i, later, carry, new=new, column=column, wide=wide):
                    if new is None:
                        density_out[i] = later
                        return carry + later
                    new.reshape(tall * width, levels)[pl.ds((TOP + i) * width + column, wide), :] = later
                    return carry

                total = advance(old, first, count, column, wide, put, total)
                if side is not None and not last:
                    advance_beyond(side, step, old, new)
                old = new
            if number < ROUNDS - 1:
                if side is None:
                    start(sideways(number + 1, TOP + DEEP, middle_rows))
                else:
                    prepare(number + 1, side)
                    start(to_side(number + 1, side))
                    start(sideways(number + 1, TOP if side == 0 else TOP + rows - DEEP, DEEP))
        if number < ROUNDS - 1:
            hear(1)
            announce(2)

    local_mean = total * (1.0 / rows)

    def square(i, carry):
        away = density_out[i] - local_mean
        return carry + away * away

    squares = lax.fori_loop(0, rows, square, jnp.zeros((columns, levels), jnp.float32), unroll=4)
    stats[0, 0] = local_mean
    stats[0, 1] = squares
    for index in range(3, len(reaches)):
        hear(index)
        announce(index + 1)
    outer = py // inner
    far_first = sorted(
        ((do, di) for do in range(outer) for di in range(inner) if do or di),
        key=lambda place: -(min(place[0], outer - place[0]) + min(place[1], inner - place[1])),
    )
    for do, di in far_first:
        step = do * inner + di
        peer = lax.rem(my // inner + do, outer) * inner + lax.rem(lax.rem(my, inner) + di, inner)
        pltpu.make_async_remote_copy(
            src_ref=stats.at[0],
            dst_ref=stats.at[step],
            send_sem=stat_sem.at[0],
            recv_sem=stat_sem.at[1],
            device_id=(peer, mx),
            device_id_type=MESH,
        ).start()
    for d, (dy, dx) in enumerate(DIRECTIONS):
        @pl.when(exists(dy, dx))
        def _():
            if dy and dx:
                count = sum(CORNER)
            elif dy:
                count = parcel(0, columns) + parcel(1, columns)
            else:
                count = 10 * rows
            settle(send_sem.at[d], count)
    others = stats.at[pl.ds(1, py - 1)]
    pltpu.make_async_copy(others, others, stat_sem.at[1]).wait()
    mean = stats[0, 0]
    for step in range(1, py):
        mean = mean + stats[step, 0]
    mean = mean * (1.0 / py)
    inside = stats[0, 1]
    between = (stats[0, 0] - mean) * (stats[0, 0] - mean)
    for step in range(1, py):
        inside = inside + stats[step, 1]
        between = between + (stats[step, 0] - mean) * (stats[step, 0] - mean)
    variance = inside * (1.0 / (rows * py)) + between * (1.0 / py)
    mean_out[...] = mean
    scale_out[...] = lax.rsqrt(variance + 0.0001)
    pltpu.make_async_copy(others, others, stat_sem.at[0]).wait()

CHUNKS = 2


def finish(density, mean, scale, anomaly_out, density_out, anomaly, sem):
    rows = density.shape[0]
    whole = pltpu.make_async_copy(density, density_out, sem.at[CHUNKS])
    whole.start()
    part = rows // CHUNKS
    copies = []
    for chunk in range(CHUNKS):
        for i in range(chunk * part, (chunk + 1) * part):
            anomaly[i] = (density[i] - mean[...]) * scale[...]
        own = pl.ds(chunk * part, part)
        copies.append(pltpu.make_async_copy(anomaly.at[own], anomaly_out.at[own], sem.at[chunk]))
        copies[-1].start()
    for copy in copies:
        copy.wait()
    whole.wait()


def per_device(py, px, inner, density, conductance, source):
    rows, columns, levels = density.shape
    tall, width = rows + 2 * TOP, columns + 2 * PAD
    vmem = pl.BlockSpec(memory_space=pltpu.VMEM)
    line = jax.ShapeDtypeStruct((columns, levels), jnp.float32)
    density, conductance, source = (pltpu.with_memory_space_constraint(x, pltpu.HBM) for x in (density, conductance, source))
    density, mean, scale = pl.pallas_call(
        functools.partial(kernel, py, px, inner),
        out_shape=[jax.ShapeDtypeStruct(density.shape, jnp.float32), line, line],
        in_specs=[pl.BlockSpec(memory_space=pltpu.HBM)] * 3,
        out_specs=[vmem] * 3,
        scratch_shapes=[
            pltpu.VMEM((4, tall, width, levels), jnp.float32),
            pltpu.VMEM((DEEP - 1, tall, width, levels), jnp.float32),
            pltpu.VMEM((2, 2, width, levels), jnp.float32),
            pltpu.VMEM((ROUNDS, 2, 4 * columns + 8, levels), jnp.float32),
            pltpu.VMEM((ROUNDS, 2, 4 * columns + 8, levels), jnp.float32),
            pltpu.VMEM((ROUNDS, 2, 2, 8, levels), jnp.float32),
            pltpu.VMEM((ROUNDS, 2, 2, 8, levels), jnp.float32),
            pltpu.VMEM((py, 2, columns, levels), jnp.float32),
            pltpu.SemaphoreType.DMA((2,)),
            pltpu.SemaphoreType.DMA((len(DIRECTIONS),)),
            pltpu.SemaphoreType.DMA((ROUNDS, 2, 3)),
            pltpu.SemaphoreType.DMA((ROUNDS, 2)),
            pltpu.SemaphoreType.DMA((2,)),
            pltpu.SemaphoreType.REGULAR((max(1, len(reaches_of(py))),)),
        ],
        compiler_params=pltpu.CompilerParams(collective_id=0, has_side_effects=True, vmem_limit_bytes=10*2**20),
    )(density, conductance, source)
    return pl.pallas_call(
        finish,
        out_shape=[jax.ShapeDtypeStruct(density.shape, jnp.float32)] * 2,
        in_specs=[vmem] * 3,
        out_specs=[pl.BlockSpec(memory_space=pltpu.HBM)] * 2,
        scratch_shapes=[pltpu.VMEM(density.shape, jnp.float32), pltpu.SemaphoreType.DMA((CHUNKS + 1,))],
        compiler_params=pltpu.CompilerParams(vmem_limit_bytes=4 * 2**20),
    )(density, mean, scale)


def solution(mesh):
    spec = P("py", "px", None)
    line = mesh.devices.reshape(mesh.shape["py"], -1)[:, 0] if mesh.axis_names[0] == "py" else []
    places = [getattr(device, "coords", (0, 0, 0))[2] for device in line]
    inner = max(1, places.count(places[0])) if places else 1
    return jax.shard_map(
        functools.partial(per_device, mesh.shape["py"], mesh.shape["px"], inner),
        mesh=mesh, in_specs=(spec,) * 3, out_specs=(spec,) * 2, check_vma=False,
    )
```

time: 25 us -> 22.4 us (0.90)
  Pallas kernels: 24.2 us -> 21.6 us
    pallas_call x1, Pallas kernels: 23.3 us -> 20.6 us  [per_device(): pl.pallas_call(functools.partial(kernel, py, px, inner), out_shape=[jax.S...]
where the time goes in v2:
time: 22.4 us; the launch traced here: 22.2 us
  Pallas kernels  21.6 us (96%)
  between operations  0.64 us (3%)
    pallas_call x1, Pallas kernels, per_device(): pl.pallas_call(functools.partial(kernel, py, px, inner), out_shape=[jax.S...  20.6 us
    pallas_call x1, Pallas kernels, per_device(): pl.pallas_call(finish, out_shape=[jax.ShapeDtypeStruct(density.shape, jnp...  0.99 us

profile of v2, /device:TPU:0, one launch (start us, length us, event | category | flops | bytes accessed | tf_op | source)
XLA Modules:
  0.0 22.2 jit_solution(9429179580845930352)
XLA Ops:
  0.6 20.6 %shard_map.50 = (f32[32,32,128]{2,1,0:T(8,128)S(1)}, f32[32,128]{1,0:T(8,128)S(1)}, f32[32,128]{1,0:T(8,128)S(1)}) custom-call(f32[32,32,128]{2,1,0:T(8,128)} %field.1, f32[32,32,128]{2,1,0:T(8,128)} %conductance.1, f32[32,32,128]{2,1,0:T(8,128)} %source.1), custom_call_target="tpu_custom_call" | custom-call | tf_op jit(solution)/shard_map/pallas_call | solution.py:378
  21.2 1.0 %shard_map.51 = (f32[32,32,128]{2,1,0:T(8,128)}, f32[32,32,128]{2,1,0:T(8,128)}) custom-call(f32[32,32,128]{2,1,0:T(8,128)S(1)} %get-tuple-element.5.density, f32[32,128]{1,0:T(8,128)S(1)} %get-tuple-element.6.mean, f32[32,128]{1,0:T(8,128)S(1)} %get-tuple-element.7.scale), custom_call_target="tpu_custom_call" | custom-call | tf_op jit(solution)/shard_map/pallas_call | solution.py:401

commit v3 on v2

v3 whole, which is shorter than its diff:
```python
import functools

import jax
import jax.numpy as jnp
from jax import lax
from jax.experimental import pallas as pl
from jax.experimental.pallas import tpu as pltpu
from jax.sharding import PartitionSpec as P

ROUNDS = 2
DEEP = 3
PAD = 4
TOP = 2
DIRECTIONS = [(-1, 0), (1, 0), (-1, -1), (-1, 1), (1, -1), (1, 1), (0, -1), (0, 1)]
MESH = pl.DeviceIdType.MESH
FIELD = (0, 3)
RATE, GAIN = 1, 2
CORNER = (5, 4)
ZONE = 2 * DEEP


def reaches_of(py):
    known, reaches = 1, []
    while known < py - 1:
        reaches.append(known)
        known *= 2
    return reaches


def parcel(number, half, columns):
    return (4 if number == 0 else 3) * (columns // 2) + (2 if number == 0 and half == 0 else 0)


def kernel(py, px, inner, field, conductance, source, density_out, mean_out, scale_out,
           arrays, work, extra, parcel_out, parcel_in, corner_out, corner_in, stats,
           load_sem, send_sem, side_sem, across_sem, stat_sem, present):
    rows, columns, levels = field.shape
    width = columns + 2 * PAD
    tall = rows + 2 * TOP
    my, mx = lax.axis_index("py"), lax.axis_index("px")
    reaches = reaches_of(py)

    def exists(dy, dx):
        here = jnp.bool_(True)
        if dy:
            here = here & ((my + dy >= 0) if dy < 0 else (my + dy < py))
        if dx:
            here = here & ((mx + dx >= 0) if dx < 0 else (mx + dx < px))
        return here

    barrier = pltpu.get_barrier_semaphore()
    expected = jnp.int32(0)
    for dy, dx in DIRECTIONS:
        there = exists(dy, dx)
        expected = expected + there.astype(jnp.int32)

        @pl.when(there)
        def _():
            pl.semaphore_signal(barrier, 1, device_id=(my + dy, mx + dx), device_id_type=MESH)

    own = pl.ds(PAD, columns)
    middle_rows = rows - 2 * DEEP
    inputs = (field, conductance, source)
    for first, count, group in ((0, DEEP, 0), (rows - DEEP, DEEP, 0), (DEEP, middle_rows, 1)):
        for i, src in enumerate(inputs):
            pltpu.make_async_copy(
                src.at[pl.ds(first, count)], arrays.at[i, pl.ds(TOP + first, count), own], load_sem.at[group]
            ).start()

    for side, dy in enumerate((-1, 1)):
        @pl.when(~exists(dy, 0))
        def _():
            parcel_in[:, side] = jnp.zeros(parcel_in.shape[:1] + parcel_in.shape[2:], jnp.float32)
        for other, dx in enumerate((-1, 1)):
            @pl.when(~exists(dy, dx))
            def _():
                for turn in range(3):
                    corner_in[turn, side, other] = jnp.zeros(corner_in.shape[3:], jnp.float32)
    for dx in (-1, 1):
        @pl.when(~exists(0, dx))
        def _():
            start = pl.ds(0 if dx < 0 else PAD + columns, PAD)
            for i in range(4):
                arrays[i, pl.ds(TOP, rows), start] = jnp.zeros((rows, PAD, levels), jnp.float32)

    edges = (TOP, TOP + rows - 1)
    beyond = (TOP - 1, TOP + rows)

    half_columns, half_levels = columns // 2, levels // 2
    low_half = lax.broadcasted_iota(jnp.int32, (half_columns, levels), 1) < half_levels

    def fold(value, half):
        first, second = value[:half_columns], value[half_columns:]
        if half == 0:
            return jnp.where(low_half, first, pltpu.roll(second, half_levels, 1))
        return jnp.where(low_half, pltpu.roll(first, half_levels, 1), second)

    def unfold(first, second=None):
        turned = pltpu.roll(first, half_levels, 1)
        if second is None:
            return first, turned
        back = pltpu.roll(second, half_levels, 1)
        return jnp.where(low_half, first, back), jnp.where(low_half, turned, second)

    def prepare(number, side, halves):
        at = FIELD[number]
        edge, inward = edges[side], 1 - 2 * side
        second, third = edge + inward, edge + 2 * inward
        outer, middle = arrays[at, edge, own], arrays[at, second, own]
        place = lax.broadcasted_iota(jnp.int32, (columns, levels), 0)
        before = jnp.where(place == 0, 0.0, pltpu.roll(middle, 1, 0))
        after = jnp.where(place == columns - 1, 0.0, pltpu.roll(middle, columns - 1, 0))
        spread = (outer + arrays[at, third, own]) + (before + after) - 4.0 * middle
        second_rate = arrays[RATE, second, own]
        later = middle + second_rate * spread + arrays[GAIN, second, own]
        rate, gain = arrays[RATE, edge, own], arrays[GAIN, edge, own]
        term = rate * middle + gain
        values = [outer, term, rate * later + gain] + ([rate] if number == 0 else [])
        for half in halves:
            out = parcel_out.at[2 * number + half, side]
            for i, value in enumerate(values):
                out[pl.ds(i * half_columns, half_columns)] = fold(value, half)
            if number == 0 and half == 0:
                out[pl.ds(4 * half_columns, 1)] = second_rate[:1]
                out[pl.ds(4 * half_columns + 1, 1)] = second_rate[columns - 1:]
        for other in range(2):
            last = columns - 1 if other else 0
            beside = columns - 2 if other else 1
            cells = corner_out.at[number + halves[0], side, other]
            cells[pl.ds(0, 1)] = outer[last:last + 1]
            cells[pl.ds(1, 1)] = outer[beside:beside + 1]
            cells[pl.ds(2, 1)] = middle[last:last + 1]
            cells[pl.ds(3, 1)] = term[last:last + 1]
            if number == 0:
                cells[pl.ds(4, 1)] = rate[last:last + 1]

    def remote(direction, src, dst, recv):
        return direction, pltpu.make_async_remote_copy(
            src_ref=src,
            dst_ref=dst,
            send_sem=send_sem.at[DIRECTIONS.index(direction)],
            recv_sem=recv,
            device_id=(my + direction[0], mx + direction[1]),
            device_id_type=MESH,
        )

    def corners(number, half, side):
        dy, there, turn = 2 * side - 1, 1 - side, number * (half + 1)
        cells = pl.ds(0, CORNER[number])
        return [remote((dy, dx), corner_out.at[turn, side, other, cells], corner_in.at[turn, there, 1 - other, cells],
                       side_sem.at[there, 4 + 2 * turn + 1 - other]) for other, dx in enumerate((-1, 1))]

    def rows_of(number, half, side):
        dy, there, size = 2 * side - 1, 1 - side, pl.ds(0, parcel(number, half, columns))
        slot = 2 * number + half
        return [remote((dy, 0), parcel_out.at[slot, side, size], parcel_in.at[slot, there, size], side_sem.at[there, slot])]

    def start(copies):
        for (dy, dx), copy in copies:
            @pl.when(exists(dy, dx))
            def _():
                copy.start()

    def wait_side(number, half, side):
        copies = rows_of(number, half, 1 - side)
        if number or not half:
            copies = copies + corners(number, half, 1 - side)
        for (dy, dx), copy in copies:
            @pl.when(exists(-dy, -dx))
            def _():
                copy.wait_recv()

    def sideways(number, group, first, count):
        out = []
        for other, dx in enumerate((-1, 1)):
            for i, reach in ((FIELD[number], 3),) + (((RATE, 2), (GAIN, 2)) if number == 0 else ()):
                from_ = PAD if dx < 0 else PAD + columns - reach
                to = PAD + columns if dx < 0 else PAD - reach
                out.append(remote((0, dx), arrays.at[i, pl.ds(first, count), pl.ds(from_, reach)],
                                  arrays.at[i, pl.ds(first, count), pl.ds(to, reach)], across_sem.at[group, 1 - other]))
        return out

    flat_all = arrays.reshape(4 * tall * width, levels)

    def settle(sem, count):
        some = flat_all.at[pl.ds(0, count)]
        pltpu.make_async_copy(some, some, sem).wait()

    def wait_across(group, count):
        for other, dx in enumerate((-1, 1)):
            @pl.when(exists(0, dx))
            def _():
                settle(across_sem.at[group, other], count)

    flat_rate = arrays.at[RATE].reshape(tall * width, levels)
    flat_gain = arrays.at[GAIN].reshape(tall * width, levels)

    def advance(old, first, count, column, wide, put, carry):
        flat = old.reshape(tall * width, levels)

        def row(i, state):
            above, middle, carry = state
            at = (first + i) * width + column
            below = flat[pl.ds(at + width, wide), :]
            sides = flat[pl.ds(at - 1, wide), :] + flat[pl.ds(at + 1, wide), :]
            spread = (above + below) + sides - 4.0 * middle
            later = middle + flat_rate[pl.ds(at, wide), :] * spread + flat_gain[pl.ds(at, wide), :]
            return middle, below, put(first - TOP + i, later, carry)

        at = first * width + column
        state = (flat[pl.ds(at - width, wide), :], flat[pl.ds(at, wide), :], carry)
        return lax.fori_loop(0, count, row, state, unroll=min(count, 4))[2]

    def advance_beyond(side, step, old, new):
        flat = old.reshape(tall * width, levels)
        at = beyond[side] * width
        inward = edges[side] * width
        middle = flat[pl.ds(at, width), :]
        sides = flat[pl.ds(at - 1, width), :] + flat[pl.ds(at + 1, width), :]
        spread = flat[pl.ds(inward, width), :] + sides - 4.0 * middle
        later = middle + flat_rate[pl.ds(at, width), :] * spread + extra[side, step]
        new.reshape(tall * width, levels)[pl.ds(at, width), :] = later

    def unpack(number, half, side):
        at, far = FIELD[number], beyond[side]
        came = [parcel_in.at[2 * number + i, side] for i in range(half + 1)]
        targets = [arrays.at[at, far], extra.at[side, 0], extra.at[side, 1]] + ([arrays.at[RATE, far]] if number == 0 else [])
        for i, target in enumerate(targets):
            parts = unfold(*[one[pl.ds(i * half_columns, half_columns)] for one in came])
            for part in range(2):
                target[pl.ds(PAD + part * half_columns, half_columns)] = parts[part]
        for other in range(2):
            cells = corner_in.at[number * (half + 1), side, other]
            last = pl.ds(PAD + columns - 1 if other else PAD, 1)
            near = pl.ds(PAD + columns if other else PAD - 1, 1)
            next_ = pl.ds(PAD + columns + 1 if other else PAD - 2, 1)
            arrays[at, far, near] = cells[pl.ds(0, 1)]
            arrays[at, far, next_] = cells[pl.ds(1, 1)]
            extra[side, 0, near] = cells[pl.ds(3, 1)]
            if number == 0:
                arrays[RATE, far, near] = cells[pl.ds(4, 1)]
            second_rate = parcel_in[0, side, pl.ds(4 * half_columns + other, 1)]
            extra[side, 1, last] = extra[side, 1, last] + (arrays[RATE, far, last] * second_rate) * cells[pl.ds(2, 1)]

    def announce(index):
        if index < len(reaches):
            for dy in (-reaches[index], reaches[index]):
                @pl.when(exists(dy, 0))
                def _():
                    pl.semaphore_signal(present.at[index], 1, device_id=(my + dy, mx), device_id_type=MESH)

    def hear(index):
        if index < len(reaches):
            count = exists(-reaches[index], 0).astype(jnp.int32) + exists(reaches[index], 0).astype(jnp.int32)
            pl.semaphore_wait(present.at[index], count)

    def steps(number, bands, side, carry):
        old = arrays.at[FIELD[number]]
        for step, (first, count) in enumerate(bands):
            last = step == DEEP - 1
            column, wide, new = 0, width, None
            if not last:
                new = work.at[step]
            else:
                column, wide = PAD, columns
                if number < ROUNDS - 1:
                    new = arrays.at[FIELD[number + 1]]

            def put(i, later, carry, new=new, column=column, wide=wide):
                if new is None:
                    density_out[i] = later
                    if carry is None:
                        return None
                    pivot, once, twice = carry
                    away = later - pivot
                    return pivot, once + away, twice + away * away
                new.reshape(tall * width, levels)[pl.ds((TOP + i) * width + column, wide), :] = later
                return carry

            if new is None and carry is None:
                advance(old, first, 1, column, wide, put, None)
                zero = jnp.zeros((columns, levels), jnp.float32)
                carry = density_out[first - TOP], zero, zero
                first, count = first + 1, count - 1
            carry = advance(old, first, count, column, wide, put, carry)
            if side is not None and not last:
                advance_beyond(side, step, old, new)
            old = new
        return carry

    def bands(part, start, growth):
        out = []
        for step in range(DEEP):
            depth = start + growth * step
            if part == "inside":
                out.append((TOP + depth, rows - 2 * depth))
            else:
                out.append((TOP if part == 0 else TOP + rows - depth, depth))
        return out

    settle(load_sem.at[0], 3 * 2 * DEEP * columns)
    for side in range(2):
        prepare(0, side, (0, 1))
    pl.semaphore_wait(barrier, expected)
    for side in range(2):
        start(corners(0, 0, side))
    for half in range(2):
        for side in range(2):
            start(rows_of(0, half, side))
    announce(0)
    settle(load_sem.at[1], 3 * middle_rows * columns)
    for side in range(2):
        start(sideways(0, 0, TOP + side * (rows - ZONE), ZONE))
    start(sideways(0, 1, TOP + ZONE, rows - 2 * ZONE))
    hear(0)
    announce(1)
    wait_across(0, 2 * ZONE * 7)
    for half in range(2):
        for side in range(2):
            wait_side(0, half, side)
            unpack(0, half, side)
            steps(0, bands(side, ZONE - 1, -1), side, ())
            prepare(1, side, (half,))
            start(corners(1, half, side) + rows_of(1, half, side))
            if half:
                start(sideways(1, 2, TOP + side * (rows - DEEP), DEEP))
        if half == 0:
            hear(1)
            announce(2)
    wait_across(1, (rows - 2 * ZONE) * 7)
    steps(0, bands("inside", ZONE - 1, -1), None, ())
    start(sideways(1, 2, TOP + DEEP, middle_rows))
    wait_across(2, rows * 3)
    within = steps(1, bands("inside", 1, 1), None, None)
    for index in range(2, len(reaches)):
        hear(index)
        announce(index + 1)
    outer = py // inner
    far_first = sorted(
        ((do, di) for do in range(outer) for di in range(inner) if do or di),
        key=lambda place: -(min(place[0], outer - place[0]) + min(place[1], inner - place[1])),
    )
    for half in range(2):
        sums = within
        for side in range(2):
            wait_side(1, half, side)
            unpack(1, half, side)
            sums = steps(1, bands(side, 1, 1), side, sums)
        pivot, once, twice = sums
        shift = once * (1.0 / rows)
        stats[half, 0, pl.ds(0, half_columns)] = fold(pivot + shift, half)
        stats[half, 0, pl.ds(half_columns, half_columns)] = fold(twice - once * shift, half)
        for do, di in far_first:
            step = do * inner + di
            peer = lax.rem(my // inner + do, outer) * inner + lax.rem(lax.rem(my, inner) + di, inner)
            pltpu.make_async_remote_copy(
                src_ref=stats.at[half, 0],
                dst_ref=stats.at[half, step],
                send_sem=stat_sem.at[2],
                recv_sem=stat_sem.at[half],
                device_id=(peer, mx),
                device_id_type=MESH,
            ).start()
    for d, (dy, dx) in enumerate(DIRECTIONS):
        @pl.when(exists(dy, dx))
        def _():
            if dy and dx:
                count = CORNER[0] + 2 * CORNER[1]
            elif dy:
                count = sum(parcel(number, half, columns) for number in range(ROUNDS) for half in range(2))
            else:
                count = 10 * rows
            settle(send_sem.at[d], count)
    means, scales = [], []
    for half in range(2):
        settle(stat_sem.at[half], (py - 1) * columns)
        came = [(stats[half, step, pl.ds(0, half_columns)], stats[half, step, pl.ds(half_columns, half_columns)])
                for step in range(py)]
        mean = came[0][0]
        for one, _ in came[1:]:
            mean = mean + one
        mean = mean * (1.0 / py)
        inside = came[0][1]
        between = (came[0][0] - mean) * (came[0][0] - mean)
        for one, squares in came[1:]:
            inside = inside + squares
            between = between + (one - mean) * (one - mean)
        variance = inside * (1.0 / (rows * py)) + between * (1.0 / py)
        means.append(mean)
        scales.append(lax.rsqrt(variance + 0.0001))
    for out, parts in ((mean_out, unfold(*means)), (scale_out, unfold(*scales))):
        for part in range(2):
            out[pl.ds(part * half_columns, half_columns)] = parts[part]
    settle(stat_sem.at[2], 2 * (py - 1) * columns)

CHUNKS = 2


def finish(density, mean, scale, anomaly_out, density_out, anomaly, sem):
    rows = density.shape[0]
    whole = pltpu.make_async_copy(density, density_out, sem.at[CHUNKS])
    whole.start()
    part = rows // CHUNKS
    copies = []
    for chunk in range(CHUNKS):
        for i in range(chunk * part, (chunk + 1) * part):
            anomaly[i] = (density[i] - mean[...]) * scale[...]
        own = pl.ds(chunk * part, part)
        copies.append(pltpu.make_async_copy(anomaly.at[own], anomaly_out.at[own], sem.at[chunk]))
        copies[-1].start()
    for copy in copies:
        copy.wait()
    whole.wait()


def per_device(py, px, inner, density, conductance, source):
    rows, columns, levels = density.shape
    tall, width = rows + 2 * TOP, columns + 2 * PAD
    vmem = pl.BlockSpec(memory_space=pltpu.VMEM)
    line = jax.ShapeDtypeStruct((columns, levels), jnp.float32)
    density, conductance, source = (pltpu.with_memory_space_constraint(x, pltpu.HBM) for x in (density, conductance, source))
    density, mean, scale = pl.pallas_call(
        functools.partial(kernel, py, px, inner),
        out_shape=[jax.ShapeDtypeStruct(density.shape, jnp.float32), line, line],
        in_specs=[pl.BlockSpec(memory_space=pltpu.HBM)] * 3,
        out_specs=[vmem] * 3,
        scratch_shapes=[
            pltpu.VMEM((4, tall, width, levels), jnp.float32),
            pltpu.VMEM((DEEP - 1, tall, width, levels), jnp.float32),
            pltpu.VMEM((2, 2, width, levels), jnp.float32),
            pltpu.VMEM((2 * ROUNDS, 2, 2 * columns + 8, levels), jnp.float32),
            pltpu.VMEM((2 * ROUNDS, 2, 2 * columns + 8, levels), jnp.float32),
            pltpu.VMEM((3, 2, 2, 8, levels), jnp.float32),
            pltpu.VMEM((3, 2, 2, 8, levels), jnp.float32),
            pltpu.VMEM((2, py, columns, levels), jnp.float32),
            pltpu.SemaphoreType.DMA((2,)),
            pltpu.SemaphoreType.DMA((len(DIRECTIONS),)),
            pltpu.SemaphoreType.DMA((2, 10)),
            pltpu.SemaphoreType.DMA((3, 2)),
            pltpu.SemaphoreType.DMA((3,)),
            pltpu.SemaphoreType.REGULAR((max(1, len(reaches_of(py))),)),
        ],
        compiler_params=pltpu.CompilerParams(collective_id=0, has_side_effects=True, vmem_limit_bytes=10*2**20),
    )(density, conductance, source)
    return pl.pallas_call(
        finish,
        out_shape=[jax.ShapeDtypeStruct(density.shape, jnp.float32)] * 2,
        in_specs=[vmem] * 3,
        out_specs=[pl.BlockSpec(memory_space=pltpu.HBM)] * 2,
        scratch_shapes=[pltpu.VMEM(density.shape, jnp.float32), pltpu.SemaphoreType.DMA((CHUNKS + 1,))],
        compiler_params=pltpu.CompilerParams(vmem_limit_bytes=4 * 2**20),
    )(density, mean, scale)


def solution(mesh):
    spec = P("py", "px", None)
    line = mesh.devices.reshape(mesh.shape["py"], -1)[:, 0] if mesh.axis_names[0] == "py" else []
    places = [getattr(device, "coords", (0, 0, 0))[2] for device in line]
    inner = max(1, places.count(places[0])) if places else 1
    return jax.shard_map(
        functools.partial(per_device, mesh.shape["py"], mesh.shape["px"], inner),
        mesh=mesh, in_specs=(spec,) * 3, out_specs=(spec,) * 2, check_vma=False,
    )
```

time: 22.4 us -> 23.3 us (1.040)
  Pallas kernels: 21.6 us -> 22.5 us
    pallas_call x1, Pallas kernels: 20.6 us -> 21.5 us  [per_device(): pl.pallas_call(functools.partial(kernel, py, px, inner), out_shape=[jax.S...]
where the time goes in v3:
time: 23.3 us; the launch traced here: 23.1 us
  Pallas kernels  22.5 us (97%)
  between operations  0.64 us (3%)
    pallas_call x1, Pallas kernels, per_device(): pl.pallas_call(functools.partial(kernel, py, px, inner), out_shape=[jax.S...  21.5 us
    pallas_call x1, Pallas kernels, per_device(): pl.pallas_call(finish, out_shape=[jax.ShapeDtypeStruct(density.shape, jnp...  0.99 us

profile of v3, /device:TPU:0, one launch (start us, length us, event | category | flops | bytes accessed | tf_op | source)
XLA Modules:
  0.0 23.1 jit_solution(16664244373405233998)
XLA Ops:
  0.6 21.5 %shard_map.50 = (f32[32,32,128]{2,1,0:T(8,128)S(1)}, f32[32,128]{1,0:T(8,128)S(1)}, f32[32,128]{1,0:T(8,128)S(1)}) custom-call(f32[32,32,128]{2,1,0:T(8,128)} %field.1, f32[32,32,128]{2,1,0:T(8,128)} %conductance.1, f32[32,32,128]{2,1,0:T(8,128)} %source.1), custom_call_target="tpu_custom_call" | custom-call | tf_op jit(solution)/shard_map/pallas_call | solution.py:422
  22.1 1.0 %shard_map.51 = (f32[32,32,128]{2,1,0:T(8,128)}, f32[32,32,128]{2,1,0:T(8,128)}) custom-call(f32[32,32,128]{2,1,0:T(8,128)S(1)} %get-tuple-element.5.density, f32[32,128]{1,0:T(8,128)S(1)} %get-tuple-element.6.mean, f32[32,128]{1,0:T(8,128)S(1)} %get-tuple-element.7.scale), custom_call_target="tpu_custom_call" | custom-call | tf_op jit(solution)/shard_map/pallas_call | solution.py:445

commit v4 on v2

--- a/solution.py
+++ b/solution.py
@@ -26,6 +26,15 @@
     return reaches
 
 
+def order_of(py, inner):
+    if (py, inner) == (8, 2):
+        return [5, 4, 3, 2, 6, 1, 7]
+    outer = py // inner
+    places = [(do, di) for do in range(outer) for di in range(inner) if do or di]
+    places.sort(key=lambda place: -(min(place[0], outer - place[0]) + min(place[1], inner - place[1])))
+    return [do * inner + di for do, di in places]
+
+
 def parcel(number, columns):
     return (4 if number == 0 else 3) * columns + (2 if number == 0 else 0)
 
@@ -47,6 +56,16 @@
             here = here & ((mx + dx >= 0) if dx < 0 else (mx + dx < px))
         return here
 
+    barrier = pltpu.get_barrier_semaphore()
+    expected = jnp.int32(0)
+    for dy, dx in DIRECTIONS:
+        there = exists(dy, dx)
+        expected = expected + there.astype(jnp.int32)
+
+        @pl.when(there)
+        def _():
+            pl.semaphore_signal(barrier, 1, device_id=(my + dy, mx + dx), device_id_type=MESH)
+
     own = pl.ds(PAD, columns)
     middle_rows = rows - 2 * DEEP
     inputs = (field, conductance, source)
@@ -55,16 +74,6 @@
             pltpu.make_async_copy(
                 src.at[pl.ds(first, count)], arrays.at[i, pl.ds(TOP + first, count), own], load_sem.at[group]
             ).start()
-
-    barrier = pltpu.get_barrier_semaphore()
-    expected = jnp.int32(0)
-    for dy, dx in DIRECTIONS:
-        there = exists(dy, dx)
-        expected = expected + there.astype(jnp.int32)
-
-        @pl.when(there)
-        def _():
-            pl.semaphore_signal(barrier, 1, device_id=(my + dy, mx + dx), device_id_type=MESH)
 
     for side, dy in enumerate((-1, 1)):
         @pl.when(~exists(dy, 0))
@@ -246,75 +255,73 @@
     settle(load_sem.at[1], 3 * middle_rows * columns)
     start(sideways(0, TOP, rows))
 
-    total = jnp.zeros((columns, levels), jnp.float32)
-    for number in range(ROUNDS):
-        wait_across(number)
-        hear(2 * number)
-        announce(2 * number + 1)
-        for part in ("inside", "low", "high"):
-            side = None if part == "inside" else (0 if part == "low" else 1)
-            if side is not None:
-                wait_side(number, side)
-                unpack(number, side)
-            old = arrays.at[FIELD[number]]
-            for step in range(DEEP):
-                last = step == DEEP - 1
-                if part == "inside":
-                    first, count = TOP + step + 1, rows - 2 * (step + 1)
-                elif part == "low":
-                    first, count = TOP, step + 1
-                else:
-                    first, count = TOP + rows - step - 1, step + 1
-                column, wide, new = 0, width, None
-                if not last:
-                    new = work.at[step]
-                else:
-                    column, wide = PAD, columns
-                    if number < ROUNDS - 1:
-                        new = arrays.at[FIELD[number + 1]]
-
-                def put(i, later, carry, new=new, column=column, wide=wide):
-                    if new is None:
-                        density_out[i] = later
-                        return carry + later
-                    new.reshape(tall * width, levels)[pl.ds((TOP + i) * width + column, wide), :] = later
-                    return carry
-
-                total = advance(old, first, count, column, wide, put, total)
-                if side is not None and not last:
-                    advance_beyond(side, step, old, new)
-                old = new
-            if number < ROUNDS - 1:
-                if side is None:
-                    start(sideways(number + 1, TOP + DEEP, middle_rows))
-                else:
-                    prepare(number + 1, side)
-                    start(to_side(number + 1, side))
-                    start(sideways(number + 1, TOP if side == 0 else TOP + rows - DEEP, DEEP))
-        if number < ROUNDS - 1:
+    def steps(number, part, carry):
+        old = arrays.at[FIELD[number]]
+        for step in range(DEEP):
+            last = step == DEEP - 1
+            depth = step + 1
+            first, count = (TOP + depth, rows - 2 * depth) if part is None else ((TOP, TOP + rows - depth)[part], depth)
+            column, wide, new = 0, width, None
+            if not last:
+                new = work.at[step]
+            else:
+                column, wide = PAD, columns
+                if number < ROUNDS - 1:
+                    new = arrays.at[FIELD[number + 1]]
+
+            def put(i, later, carry, new=new, column=column, wide=wide):
+                if new is None:
+                    density_out[i] = later
+                    if carry is None:
+                        return None
+                    pivot, once, twice = carry
+                    away = later - pivot
+                    return pivot, once + away, twice + away * away
+                new.reshape(tall * width, levels)[pl.ds((TOP + i) * width + column, wide), :] = later
+                return carry
+
+            if new is None and carry is None:
+                advance(old, first, 1, column, wide, put, None)
+                zero = jnp.zeros((columns, levels), jnp.float32)
+                carry = density_out[first - TOP], zero, zero
+                first, count = first + 1, count - 1
+            carry = advance(old, first, count, column, wide, put, carry)
+            if part is not None and not last:
+                advance_beyond(part, step, old, new)
+            old = new
+        return carry
+
+    hear(0)
+    announce(1)
+    wait_across(0)
+    steps(0, None, ())
+    start(sideways(1, TOP + DEEP, middle_rows))
+    for side in range(2):
+        wait_side(0, side)
+        unpack(0, side)
+        steps(0, side, ())
+        prepare(1, side)
+        start(to_side(1, side))
+        start(sideways(1, TOP if side == 0 else TOP + rows - DEEP, DEEP))
+        if side == 0:
             hear(1)
             announce(2)
-
-    local_mean = total * (1.0 / rows)
-
-    def square(i, carry):
-        away = density_out[i] - local_mean
-        return carry + away * away
-
-    squares = lax.fori_loop(0, rows, square, jnp.zeros((columns, levels), jnp.float32), unroll=4)
-    stats[0, 0] = local_mean
-    stats[0, 1] = squares
-    for index in range(3, len(reaches)):
+    wait_across(1)
+    sums = steps(1, None, None)
+    for index in range(2, len(reaches)):
         hear(index)
         announce(index + 1)
-    outer = py // inner
-    far_first = sorted(
-        ((do, di) for do in range(outer) for di in range(inner) if do or di),
-        key=lambda place: -(min(place[0], outer - place[0]) + min(place[1], inner - place[1])),
-    )
-    for do, di in far_first:
-        step = do * inner + di
-        peer = lax.rem(my // inner + do, outer) * inner + lax.rem(lax.rem(my, inner) + di, inner)
+    for side in range(2):
+        wait_side(1, side)
+        unpack(1, side)
+        sums = steps(1, side, sums)
+    pivot, once, twice = sums
+    shift = once * (1.0 / rows)
+    stats[0, 0] = pivot + shift
+    stats[0, 1] = twice - once * shift
+    for step in order_of(py, inner):
+        do, di = step // inner, step % inner
+        peer = lax.rem(my // inner + do, py // inner) * inner + lax.rem(lax.rem(my, inner) + di, inner)
         pltpu.make_async_remote_copy(
             src_ref=stats.at[0],
             dst_ref=stats.at[step],

time: 22.4 us -> 22.1 us (0.987)
  Pallas kernels: 21.6 us -> 21.3 us
    pallas_call x1, Pallas kernels: 20.6 us -> 20.3 us  [per_device(): pl.pallas_call(functools.partial(kernel, py, px, inner), out_shape=[jax.S...]
where the time goes in v4:
time: 22.1 us; the launch traced here: 21.9 us
  Pallas kernels  21.3 us (96%)
  between operations  0.64 us (3%)
    pallas_call x1, Pallas kernels, per_device(): pl.pallas_call(functools.partial(kernel, py, px, inner), out_shape=[jax.S...  20.3 us
    pallas_call x1, Pallas kernels, per_device(): pl.pallas_call(finish, out_shape=[jax.ShapeDtypeStruct(density.shape, jnp...  0.99 us

profile of v4, /device:TPU:0, one launch (start us, length us, event | category | flops | bytes accessed | tf_op | source)
XLA Modules:
  0.0 21.9 jit_solution(7619072926997273511)
XLA Ops:
  0.6 20.3 %shard_map.50 = (f32[32,32,128]{2,1,0:T(8,128)S(1)}, f32[32,128]{1,0:T(8,128)S(1)}, f32[32,128]{1,0:T(8,128)S(1)}) custom-call(f32[32,32,128]{2,1,0:T(8,128)} %field.1, f32[32,32,128]{2,1,0:T(8,128)} %conductance.1, f32[32,32,128]{2,1,0:T(8,128)} %source.1), custom_call_target="tpu_custom_call" | custom-call | tf_op jit(solution)/shard_map/pallas_call | solution.py:385
  20.9 1.0 %shard_map.51 = (f32[32,32,128]{2,1,0:T(8,128)}, f32[32,32,128]{2,1,0:T(8,128)}) custom-call(f32[32,32,128]{2,1,0:T(8,128)S(1)} %get-tuple-element.5.density, f32[32,128]{1,0:T(8,128)S(1)} %get-tuple-element.6.mean, f32[32,128]{1,0:T(8,128)S(1)} %get-tuple-element.7.scale), custom_call_target="tpu_custom_call" | custom-call | tf_op jit(solution)/shard_map/pallas_call | solution.py:408
